TPU v7x, 32 devices: a whole 2x2x4 slice. The times are simulated.
32 devices in a mesh: dp: 4 (over y, x), seq: 8 (over z, core).
Axes of the slice: x: 2, y: 2, z: 4, core: 2. Of those that a mesh axis runs over, the one named last changes fastest.
Arguments:
- hidden_in: bfloat16 [4, 2048, 1536], P('dp', 'seq'), may hold values from -6 to 6
- pre_gain: bfloat16 [1536], P('dp'), may hold values from 0.5 to 1.5
- in_weight: bfloat16 [1536, 6448], P('dp'), may hold values from -0.15625 to 0.15625
- conv_x_weight: float32 [4, 3072], replicated, may hold values from -3 to 3
- conv_x_bias: float32 [3072], replicated, may hold values from -3 to 3
- conv_bc_weight: float32 [4, 256], replicated, may hold values from -3 to 3
- conv_bc_bias: float32 [256], replicated, may hold values from -3 to 3
- dt_bias: float32 [48], replicated, may hold values from -5 to -2
- a_log: float32 [48], replicated, may hold values from -4.5 to 2.8
- skip: float32 [48], replicated, may hold values from 0.5 to 1.5
- norm_gain: bfloat16 [3072], P('dp'), may hold values from 0.5 to 1.5
- out_weight: bfloat16 [3072, 1536], P('dp'), may hold values from -0.109375 to 0.109375
- output_gradient: bfloat16 [4, 2048, 1536], P('dp', 'seq'), may hold values from -6 to 6
Outputs:
- output: float32 [4, 2048, 1536], P('dp', 'seq')
- input_grad: float32 [4, 2048, 1536], P('dp', 'seq')
- pre_gain_grad: float32 [1536], P('dp')
- in_weight_grad: float32 [1536, 6448], P('dp')
- conv_x_weight_grad: float32 [4, 3072], replicated
- conv_x_bias_grad: float32 [3072], replicated
- conv_bc_weight_grad: float32 [4, 256], replicated
- conv_bc_bias_grad: float32 [256], replicated
- dt_bias_grad: float32 [48], replicated
- a_log_grad: float32 [48], replicated
- skip_grad: float32 [48], replicated
- norm_gain_grad: float32 [3072], P('dp')
- out_weight_grad: float32 [3072, 1536], P('dp')
All inputs are finite; a program needn't handle non-finite values.
Results may differ from a plain program's by a relative error of at most 0.008.
The roundings to bfloat16 on the way count: a program that leaves them out, or rounds other values in their place, can miss the bound.
Values may be sent and summed in bfloat16 or wider, within the bound.
A program may use at most 256 MiB of HBM per device.

v0:
```python
import functools
import types

import jax
import jax.numpy as jnp
from jax import lax
from jax.experimental import pallas as pl
from jax.experimental.pallas import tpu as pltpu
from jax.sharding import Mesh
from jax.sharding import PartitionSpec as P

EPSILON = 1e-05
BLOCK = 256
HALO = 16
F32 = jnp.float32
BF16 = jnp.bfloat16
NN = ((1,), (0,))
NT = ((1,), (1,))
TN = ((0,), (0,))


def mm(a, b, dims=NN):
    return lax.dot_general(
        a.astype(BF16), b.astype(BF16), (dims, ((), ())), preferred_element_type=F32
    )


def split(a):
    high = a.astype(BF16)
    return high, (a - high.astype(F32)).astype(BF16)


def mm3(a, b, dims=NN):
    ah, al = split(a)
    bh, bl = split(b)
    return mm(ah, bh, dims) + (mm(ah, bl, dims) + mm(al, bh, dims))


def mm_exact(a, b, dims=NN):
    b0 = b.astype(BF16)
    r1 = b - b0.astype(F32)
    b1 = r1.astype(BF16)
    b2 = (r1 - b1.astype(F32)).astype(BF16)
    return mm(a, b0, dims) + (mm(a, b1, dims) + mm(a, b2, dims))


def mm_sum(a, b, dims=NN):
    ah, al = split(a)
    return mm(ah, b, dims) + mm(al, b, dims)


def sigmoid(v):
    return 1.0 / (1.0 + jnp.exp(-v))


def lane_mask(width, first):
    lane = lax.broadcasted_iota(jnp.int32, (1, 128), 1)
    return (lane < 64) if first else (lane >= 64)


def expand(v, pair):
    lane = lax.broadcasted_iota(jnp.int32, (1, 128), 1)
    return jnp.where(lane < 64, v[:, 2 * pair : 2 * pair + 1], v[:, 2 * pair + 1 : 2 * pair + 2])


def lower_mask():
    return lax.broadcasted_iota(jnp.int32, (BLOCK, BLOCK), 0) >= lax.broadcasted_iota(
        jnp.int32, (BLOCK, BLOCK), 1
    )


def head_indicator(pair):
    row = lax.broadcasted_iota(jnp.int32, (128, 128), 0)
    col = lax.broadcasted_iota(jnp.int32, (128, 128), 1)
    return (col == 2 * pair + row // 64).astype(BF16)


def conv_block(p_ref, row, col, w_ref, b_ref, wcol):
    raw = p_ref[pl.ds(row, BLOCK + HALO), col : col + 128].astype(F32)
    shifted = [raw[HALO - 3 + k : HALO - 3 + k + BLOCK] for k in range(4)]
    pre = b_ref[0:1, wcol : wcol + 128]
    for k in range(4):
        pre = pre + w_ref[k : k + 1, wcol : wcol + 128] * shifted[k]
    return pre, shifted


def run_hooks(hooks, at):
    for index, hook in hooks.items():
        pl.when(at == index)(hook)


def prep_pass(width, px_ref, pt_ref, pd_ref, wx_ref, bx_ref, wb_ref, bb_ref, dtb_ref, alog_ref,
              xs_ref, bc_ref, dt_ref, cum_ref, fin_ref, hooks):
    blocks = xs_ref.shape[0] // BLOCK
    rate = -jnp.exp(alog_ref[...])
    fin_ref[...] = jnp.zeros_like(fin_ref)

    def step(b, carry):
        row = pl.multiple_of(b * BLOCK, BLOCK)
        for c in range(2):
            pre, _ = conv_block(pt_ref, row, 128 * c, wb_ref, bb_ref, 128 * c)
            bc_ref[pl.ds(row, BLOCK), 128 * c : 128 * c + 128] = pre * sigmoid(pre)
        raw = pd_ref[pl.ds(row + HALO, BLOCK), :].astype(F32)
        raw = raw + dtb_ref[...]
        dt = jnp.maximum(raw, 0.0) + jnp.log1p(jnp.exp(-jnp.abs(raw)))
        cum = mm_exact(lower_mask().astype(F32), dt * rate)
        dt_ref[pl.ds(row, BLOCK), :] = dt
        cum_ref[pl.ds(row, BLOCK), :] = cum
        last = cum[BLOCK - 1 : BLOCK, :]
        weight = dt * jnp.exp(last - cum)
        decay = jnp.exp(last)
        keys_t = bc_ref[pl.ds(row, BLOCK), 0:128].T
        for pair in range(width // 128):
            cols = slice(128 * pair, 128 * pair + 128)
            pre, _ = conv_block(px_ref, row, 128 * pair, wx_ref, bx_ref, 128 * pair)
            xs = pre * sigmoid(pre)
            xs_ref[pl.ds(row, BLOCK), cols] = xs
            fin_ref[:, cols] = fin_ref[:, cols] * expand(decay, pair) + mm3(
                keys_t, xs * expand(weight, pair)
            )
        run_hooks(hooks, b)
        return carry

    lax.fori_loop(0, blocks, step, 0)


def inside_pass(width, xs_ref, bc_ref, dt_ref, cum_ref, yl_ref, hooks):
    def step(b, carry):
        rows = pl.ds(pl.multiple_of(b * BLOCK, BLOCK), BLOCK)
        dt, cum = dt_ref[rows, :], cum_ref[rows, :]
        cum_t = cum.T
        scores = mm3(bc_ref[rows, 128:256], bc_ref[rows, 0:128], NT)
        mask = lower_mask()
        for pair in range(width // 128):
            cols = slice(128 * pair, 128 * pair + 128)
            stepped = xs_ref[rows, cols] * expand(dt, pair)
            y = jnp.zeros((BLOCK, 128), F32)
            for half in range(2):
                h = 2 * pair + half
                spread = cum[:, h : h + 1] - cum_t[h : h + 1, :]
                table = jnp.exp(jnp.where(mask, spread, -1e30))
                part = jnp.where(lane_mask(128, half == 0), stepped, 0.0)
                y = y + mm3(scores * table, part)
            yl_ref[rows, cols] = y
        run_hooks(hooks, b)
        return carry

    lax.fori_loop(0, xs_ref.shape[0] // BLOCK, step, 0)


def outside_pass(
    width, xs_ref, bc_ref, dt_ref, cum_ref, skip_ref, y_ref, yl_ref, states_ref, s_ref, hooks
):
    def step(b, carry):
        rows = pl.ds(pl.multiple_of(b * BLOCK, BLOCK), BLOCK)
        dt, cum = dt_ref[rows, :], cum_ref[rows, :]
        last = cum[BLOCK - 1 : BLOCK, :]
        grow, decay = jnp.exp(cum), jnp.exp(last)
        weight = dt * jnp.exp(last - cum)
        queries = bc_ref[rows, 128:256]
        keys_t = bc_ref[rows, 0:128].T
        for pair in range(width // 128):
            cols = slice(128 * pair, 128 * pair + 128)
            xs = xs_ref[rows, cols]
            state = s_ref[:, cols]
            states_ref[b, :, cols] = state
            y = yl_ref[rows, cols] + expand(grow, pair) * mm3(queries, state)
            s_ref[:, cols] = state * expand(decay, pair) + mm3(keys_t, xs * expand(weight, pair))
            yl_ref[rows, cols] = y
            y_ref[rows, cols] = (y + skip_ref[0:1, cols] * xs).astype(BF16)
        run_hooks(hooks, b)
        return carry

    lax.fori_loop(0, xs_ref.shape[0] // BLOCK, step, 0)


MESH = pl.DeviceIdType.MESH


def bits_of(count):
    return [1 << i for i in range(count.bit_length() - 1)]


def bit_at(index, bit):
    return (index // bit) % 2


def flip(index, bits):
    for bit in bits:
        index = index + bit * (1 - 2 * bit_at(index, bit))
    return index


def subsets(bits):
    found = [frozenset()]
    for bit in bits:
        found = found + [f | {bit} for f in found]
    return found


class Links:
    def __init__(self, send, recv):
        self.send, self.recv, self.count, self.open = send, recv, 0, []

    def make(self, src, dst, target):
        index, self.count = self.count, self.count + 1
        return pltpu.make_async_remote_copy(
            src_ref=src, dst_ref=dst, send_sem=self.send.at[index], recv_sem=self.recv.at[index],
            device_id=target, device_id_type=MESH,
        )

    def stage(self, copies, after=None):
        def begin():
            for copy in copies:
                copy.start()
                self.open.append(lambda copy=copy: copy.wait_send())

        def end():
            for copy in copies:
                copy.wait_recv()
            if after is not None:
                after()

        return begin, end

    def stage_if(self, copy, sends, takes):
        def left():
            pl.when(sends)(copy.wait_send)

        def begin():
            pl.when(sends)(copy.start)
            self.open.append(left)

        def end():
            pl.when(takes)(copy.wait_recv)

        return begin, end

    def drain(self):
        for left in self.open:
            left()
        self.open = []


def meet(targets):
    barrier = pltpu.get_barrier_semaphore()
    for target in targets:
        pl.semaphore_signal(barrier, inc=1, device_id=target, device_id_type=MESH)
    pl.semaphore_wait(barrier, len(targets))


def neighbours(axis):
    me = lax.axis_index(axis)
    return [{axis: flip(me, (bit,))} for bit in bits_of(lax.axis_size(axis))]


class Flow:
    def __init__(self, links, stages):
        self.links, self.stages, self.at, self.sent = links, stages, -1, []

    def go(self):
        if 0 <= self.at < len(self.stages):
            self.stages[self.at][1]()
        self.at += 1
        if self.at < len(self.stages):
            before = len(self.links.open)
            self.stages[self.at][0]()
            self.sent += self.links.open[before:]

    def drain(self):
        for left in self.sent:
            left()
        done = {id(left) for left in self.sent}
        self.links.open = [left for left in self.links.open if id(left) not in done]
        self.sent = []

    def finish(self):
        while self.at < len(self.stages):
            self.go()


def step(*flows):
    for flow in flows:
        flow.go()


def finish(*flows):
    while any(flow.at < len(flow.stages) for flow in flows):
        for flow in flows:
            if flow.at < len(flow.stages):
                flow.go()


def add_rows(out, a, b):
    rows = out.shape[0]
    step = 16 if rows % 16 == 0 else 8

    @pl.loop(0, rows // step)
    def _(i):
        at = pl.ds(pl.multiple_of(i * step, step), step)
        out[at, :] = (a[at, :].astype(F32) + b[at, :].astype(F32)).astype(out.dtype)


def gather_stages(links, axis, order, own, slot):
    me = lax.axis_index(axis)
    held, stages = [frozenset()], []
    for bit in order:
        target = {axis: flip(me, (bit,))}
        stages.append(
            links.stage([
                links.make(slot(flip(me, f)) if f else own, slot(flip(me, f)), target) for f in held
            ])
        )
        held = held + [f | {bit} for f in held]
    return stages


def reduce_stages(links, axis, order, source, inbox, final=None):
    me = lax.axis_index(axis)
    base, stages = 0, []
    blocks = {f: source(flip(me, f)) for f in subsets(order)}
    for stage, bit in enumerate(order):
        keep = subsets(order[stage + 1 :])
        target = {axis: flip(me, (bit,))}
        boxes = [inbox(base + k) for k in range(len(keep))]
        outs = [final] if final is not None and stage == len(order) - 1 else boxes
        copies = [links.make(blocks[f | {bit}], box, target) for f, box in zip(keep, boxes)]

        def after(mine=[blocks[f] for f in keep], boxes=boxes, outs=outs):
            for a, b, out in zip(mine, boxes, outs):
                add_rows(out, a, b)

        stages.append(links.stage(copies, after))
        blocks = dict(zip(keep, outs))
        base += len(keep)
    return stages


def spread_stages(links, order, block):
    d, q = lax.axis_index("dp"), lax.axis_index("quad")
    away = {bit: bit_at(d, bit) != bit_at(q, bit) for bit in order}
    stages = []
    for stage, bit in enumerate(order):
        reached = jnp.bool_(True)
        for later in order[stage + 1 :]:
            reached = jnp.logical_and(reached, jnp.logical_not(away[later]))
        holder = jnp.logical_and(reached, jnp.logical_not(away[bit]))
        taker = jnp.logical_and(reached, away[bit])
        copy = links.make(block, block, {"dp": flip(d, (bit,))})
        stages.append(links.stage_if(copy, holder, taker))
    return stages


def leave_pass(width, bc_ref, cum_ref, gy_ref, out_ref):
    blocks = gy_ref.shape[0] // BLOCK
    out_ref[...] = jnp.zeros_like(out_ref)

    def step(i, carry):
        rows = pl.ds(pl.multiple_of((blocks - 1 - i) * BLOCK, BLOCK), BLOCK)
        cum = cum_ref[rows, :]
        grow, decay = jnp.exp(cum), jnp.exp(cum[BLOCK - 1 : BLOCK, :])
        queries_t = bc_ref[rows, 128:256].T
        for pair in range(width // 128):
            cols = slice(128 * pair, 128 * pair + 128)
            dy = gy_ref[rows, cols].astype(F32)
            out_ref[:, cols] = out_ref[:, cols] * expand(decay, pair) + mm3(
                queries_t, expand(grow, pair) * dy
            )
        return carry

    lax.fori_loop(0, blocks, step, 0)


def back_inside_pass(width, r, hooks):
    def step(b, carry):
        rows = pl.ds(pl.multiple_of(b * BLOCK, BLOCK), BLOCK)
        dt, cum = r.dt[rows, :], r.cum[rows, :]
        cum_t = cum.T
        keys, queries = r.bc[rows, 0:128], r.bc[rows, 128:256]
        scores = mm3(queries, keys, NT)
        mask = lower_mask()
        r.dscore[...] = jnp.zeros_like(r.dscore)
        for pair in range(width // 128):
            cols = slice(128 * pair, 128 * pair + 128)
            stepped, stepped_low = split(r.xs[rows, cols] * expand(dt, pair))
            dy = r.y[rows, cols].astype(F32)
            dstep = jnp.zeros((BLOCK, 128), F32)
            for half in range(2):
                h = 2 * pair + half
                spread = cum[:, h : h + 1] - cum_t[h : h + 1, :]
                table = jnp.exp(jnp.where(mask, spread, -1e30))
                part = jnp.where(lane_mask(128, half == 0), dy, 0.0).astype(BF16)
                dmix = mm(part, stepped, NT) + mm(part, stepped_low, NT)
                r.dscore[...] += dmix * table
                high, low = split(scores * table)
                dstep = dstep + (mm(high, part, TN) + mm(low, part, TN))
            r.gm[rows, cols] = dstep
        r.dbc[rows, 0:128] = mm3(r.dscore[...], queries, TN)
        r.dbc[rows, 128:256] = mm3(r.dscore[...], keys)
        run_hooks(hooks, b)
        return carry

    lax.fori_loop(0, r.y.shape[0] // BLOCK, step, 0)


def back_outside_pass(width, r, hooks):
    blocks = r.y.shape[0] // BLOCK
    rate = -jnp.exp(r.alog[...])
    r.heads[...] = jnp.zeros_like(r.heads)

    def step(i, carry):
        b = blocks - 1 - i
        row = pl.multiple_of(b * BLOCK, BLOCK)
        rows = pl.ds(row, BLOCK)
        dt, cum = r.dt[rows, :], r.cum[rows, :]
        last = cum[BLOCK - 1 : BLOCK, :]
        grow, decay, tail = jnp.exp(cum), jnp.exp(last), jnp.exp(last - cum)
        keys, queries = r.bc[rows, 0:128], r.bc[rows, 128:256]
        queries_t = queries.T
        dkeys, dqueries = r.dbc[rows, 0:128], r.dbc[rows, 128:256]
        dcum = jnp.zeros((BLOCK, 128), F32)
        ddt = jnp.zeros((BLOCK, 128), F32)
        dlast = jnp.zeros((8, 128), F32)
        dskip = jnp.zeros((8, 128), F32)
        for pair in range(width // 128):
            cols = slice(128 * pair, 128 * pair + 128)
            xs = r.xs[rows, cols]
            dt_e = expand(dt, pair)
            stepped = xs * dt_e
            dy = r.y[rows, cols].astype(F32)
            state, ds = r.states[b, :, cols], r.ds[:, cols]
            tail_e = expand(tail, pair)
            carried = mm3(keys, ds) * tail_e
            dstep = r.gm[rows, cols] + carried
            dkeys = dkeys + mm3(stepped * tail_e, ds, NT)
            grown = expand(grow, pair) * dy
            dqueries = dqueries + mm3(grown, state, NT)
            decay_e = expand(decay, pair)
            ends = jnp.sum(stepped * carried, 0, keepdims=True) + decay_e * jnp.sum(
                ds * state, 0, keepdims=True
            )
            r.ds[:, cols] = ds * decay_e + mm3(queries_t, grown)
            dxs = dstep * dt_e + r.skip[0:1, cols] * dy
            which = head_indicator(pair)
            ddt = ddt + mm_sum(dstep * xs, which)
            dcum = dcum + mm_sum(dy * r.yl[rows, cols] - stepped * dstep, which)
            dlast = dlast + mm_sum(jnp.broadcast_to(ends, (8, 128)), which)
            skips = jnp.sum(dy * xs, 0, keepdims=True)
            dskip = dskip + mm_sum(jnp.broadcast_to(skips, (8, 128)), which)
            pre, shifted = conv_block(r.px, row, 128 * pair, r.wxc, r.bxc, 128 * pair)
            sig = sigmoid(pre)
            dpre = dxs * sig * (1.0 + pre * (1.0 - sig))
            r.xs[rows, cols] = dpre
            for k in range(4):
                r.sx[k : k + 1, cols] += jnp.sum(dpre * shifted[k], 0, keepdims=True)
            r.sx[4:5, cols] += jnp.sum(dpre, 0, keepdims=True)
        at_end = lax.broadcasted_iota(jnp.int32, (BLOCK, 128), 0) == BLOCK - 1
        dcum = dcum + jnp.where(at_end, dlast[0:1], 0.0)
        dlog = mm_exact(lower_mask().astype(F32), dcum, TN)
        raw = r.pd[pl.ds(row + HALO, BLOCK), :].astype(F32)
        draw = (ddt + dlog * rate) * sigmoid(raw + r.dtb[...])
        r.gdt[rows, :] = draw.astype(BF16)
        r.heads[0:1, :] += jnp.sum(draw, 0, keepdims=True)
        r.heads[1:2, :] += jnp.sum(dlog * dt, 0, keepdims=True) * rate
        r.heads[2:3, :] += dskip[0:1]
        for c, grad in enumerate((dkeys, dqueries)):
            cols = slice(128 * c, 128 * c + 128)
            pre, shifted = conv_block(r.pt, row, 128 * c, r.wbc, r.bbc, 128 * c)
            sig = sigmoid(pre)
            dpre = grad * sig * (1.0 + pre * (1.0 - sig))
            r.dbc[rows, cols] = dpre
            for k in range(4):
                r.sb[k : k + 1, cols] += jnp.sum(dpre * shifted[k], 0, keepdims=True)
            r.sb[4:5, cols] += jnp.sum(dpre, 0, keepdims=True)
        run_hooks(hooks, i)
        return carry

    lax.fori_loop(0, blocks, step, 0)


INPUTS = (
    "win", "wo_in", "hid_in", "og_in", "gain_in", "wxc", "bxc", "wbc", "bbc", "dtb", "alog", "skip",
)
OUTPUTS = (
    "in_out", "out_out", "op_own", "gn_own", "cxw", "cxb", "norm", "cbw", "cbb", "head", "pre", "pre_gain",
)
SCRATCH = (
    "wz", "wx", "wt", "wo", "xn", "og", "hid", "px", "pt", "pd", "xs", "bc", "dt", "cum", "y", "yl", "states", "z", "gm", "mixed", "dbc", "gdt", "bcs", "bcbox", "bcall", "tail", "wtail", "grad", "gradt", "zbox", "zpair", "xpair", "tbox", "tpair", "obox", "opair", "opbox", "ttot", "tstage", "gain", "halo", "fin", "enter", "ds", "stat", "statbox", "dscore", "heads", "sx", "sb", "sp", "sxbox", "sbbox", "spbox", "sxall", "sball", "spall", "hx", "hb", "dsin", "send", "recv", "local",
)


def block_kernel(width, own_heads, heads, *refs):
    r = types.SimpleNamespace(**dict(zip((*INPUTS, *OUTPUTS, *SCRATCH), refs, strict=True)))
    d, q, p = lax.axis_index("dp"), lax.axis_index("quad"), lax.axis_index("pair")
    dps, quads = lax.axis_size("dp"), lax.axis_size("quad")
    tokens, piece, model = r.y.shape[0], r.hid.shape[1], r.hid.shape[2]
    inner, share, state2 = width * quads, model // dps, r.bc.shape[1]
    bc_cols = state2 // quads
    links = Links(r.send, r.recv)
    dp_bits, up = bits_of(dps), bits_of(quads)
    orders, down = (dp_bits, dp_bits[::-1]), up[::-1]
    other, swapped = {"pair": flip(p, (1,))}, {"dp": q, "quad": d}
    near = neighbours("dp") + neighbours("quad") + neighbours("pair")
    sides = ((0, width // 2), (width // 2, width // 2))
    tail_rows = r.win.shape[0] - 2 * inner
    cut = tail_rows // 32 * 16 + 16
    tail_sides = ((0, cut), (cut, tail_rows - cut))
    lane_row = lax.broadcasted_iota(jnp.int32, (128, 128), 0)
    lane_col = lax.broadcasted_iota(jnp.int32, (128, 128), 1)
    first_half, second_half = p == 0, p > 0

    @pl.when(d == q)
    def _():
        meet(near)

    @pl.when(d != q)
    def _():
        meet([*near, swapped])

    def win_rows(base, at, size):
        return r.win.at[pl.ds(pl.multiple_of(base + q * width + at, 16), size)]

    def tail_source(at, size):
        return r.win.at[pl.ds(2 * inner + at, size)]

    def weights(source, out, parts):
        return [
            Flow(links, gather_stages(
                links, "dp", order, source(at, size),
                lambda i, at=at, size=size: out.at[i, pl.ds(at, size)],
            ))
            for order, (at, size) in zip(orders, parts)
        ]

    gain_flow = Flow(links, gather_stages(links, "dp", dp_bits, r.gain_in, lambda i: r.gain.at[i]))
    hid_flow = Flow(links, gather_stages(links, "quad", down, r.hid_in, lambda i: r.hid.at[i]))
    og_flow = Flow(links, gather_stages(links, "quad", down, r.og_in, lambda i: r.og.at[i]))
    wt_flows = weights(tail_source, r.wt, tail_sides)
    wx_flows = weights(lambda at, size: win_rows(inner, at, size), r.wx, sides)
    wz_flows = weights(lambda at, size: win_rows(0, at, size), r.wz, sides)
    parts = 4
    wo_flows = [
        Flow(links, spread_stages(links, dp_bits[::-1], r.wo.at[pl.ds(k * (width // parts), width // parts)]))
        for k in range(parts)
    ]
    tail = r.hid.at[quads - 1, pl.ds(piece - HALO, HALO)]
    halo_flow = Flow(links, [links.stage_if(links.make(tail, r.halo, other), first_half, second_half)])
    state_flow = Flow(links, [links.stage_if(links.make(r.fin, r.enter, other), first_half, second_half)])
    ds_flow = Flow(links, [links.stage_if(links.make(r.fin, r.dsin, other), second_half, first_half)])
    edge_flows = [
        Flow(links, [links.stage_if(links.make(a.at[pl.ds(0, 8)], b, other), second_half, first_half)])
        for a, b in ((r.xs, r.hx), (r.dbc, r.hb))
    ]
    stat_flow = Flow(links, [
        links.stage(
            [links.make(r.stat.at[k], r.statbox.at[k], {"quad": flip(q, (bit,))})],
            lambda k=k: r.stat.at[k + 1].__setitem__(..., r.stat[k] + r.statbox[k]),
        )
        for k, bit in enumerate(up)
    ])
    kept = []

    def keeper(own, place, index):
        return pltpu.make_async_copy(own, place, r.local.at[index])

    def in_flow(h, at, size, part_ref, box, pair_box, slot, index):
        rows = pl.ds(at, size)
        stages = reduce_stages(
            links, "dp", orders[h], lambda i: part_ref.at[i, rows], lambda k: box.at[k, rows]
        )
        mine, own = box.at[dps - 2, rows], pair_box.at[rows]
        keep = keeper(own, slot(q), index)

        def after():
            add_rows(own, mine, own)
            keep.start()
            kept.append(keep)

        stages.append(links.stage([links.make(mine, own, other)], after))
        return Flow(links, stages + gather_stages(links, "quad", down, own, slot))

    def columns_slot(base, at, size):
        return lambda i: r.in_out.at[pl.ds(pl.multiple_of(base + i * width + at, 16), size)]

    def out_flow(h):
        half = model // 2
        part, size = pl.ds(h * half, half), width // dps
        stages = reduce_stages(
            links, "dp", orders[h],
            lambda i: r.wo.at[pl.ds(pl.multiple_of(i * size, 16), size), part],
            lambda k: r.obox.at[h, k],
        )
        mine, whole = r.obox.at[h, dps - 2], r.opair.at[h]
        place = r.out_out.at[d, :, part]
        stages.append(
            links.stage([links.make(mine, whole, other)], lambda: add_rows(whole, mine, whole))
        )
        near_copy = pltpu.make_async_copy(whole, place, r.local.at[14 + h])
        far_copy = links.make(whole, place, swapped)

        def begin():
            pl.when(d == q)(near_copy.start)
            pl.when(d != q)(far_copy.start)

        def end():
            pl.when(d == q)(near_copy.wait)
            pl.when(d != q)(far_copy.wait)

        stages.append((begin, end))
        return Flow(links,
            stages
            + gather_stages(
                links, "quad", down, r.out_out.at[q, :, part], lambda i: r.out_out.at[i, :, part]
            )
        )

    def row_sum_flow(source, box, final):
        return Flow(links, reduce_stages(
            links, "quad", up, lambda i: source.at[i], lambda k: box.at[k], final
        ))

    def small_flow(mine, box, every):
        current, stages = mine, []
        steps = [("dp", bit) for bit in dp_bits] + [("pair", 1)]
        for k, (axis, bit) in enumerate(steps):
            target = {axis: flip(lax.axis_index(axis), (bit,))}
            out = box.at[k] if k < len(steps) - 1 else every.at[q]

            def after(out=out, current=current, k=k):
                out[...] = current[...] + box[k]

            stages.append(links.stage([links.make(current, box.at[k], target)], after))
            current = out
        return Flow(links,
            stages + gather_stages(links, "quad", down, every.at[q], lambda i: every.at[i])
        )

    z_flows = [
        in_flow(h, at, size, r.grad, r.zbox, r.zpair, columns_slot(0, at, size), 7 + h)
        for h, (at, size) in enumerate(sides)
    ]
    x_flows = [
        in_flow(h, at, size, r.grad, r.zbox, r.xpair, columns_slot(inner, at, size), 9 + h)
        for h, (at, size) in enumerate(sides)
    ]
    t_flow = in_flow(0, 0, 128, r.gradt, r.tbox, r.tpair, lambda i: r.ttot.at[i], 11)
    out_flows = [out_flow(0), out_flow(1)]
    op_flow = row_sum_flow(r.hid, r.opbox, r.op_own)
    gn_flow = row_sum_flow(r.og, r.opbox, r.gn_own)
    bc_flow = Flow(links,
        reduce_stages(links, "quad", up, lambda i: r.bcs.at[i], lambda k: r.bcbox.at[k], r.bcall.at[q])
        + gather_stages(links, "quad", down, r.bcall.at[q], lambda i: r.bcall.at[i])
    )
    sx_flow, sb_flow, sp_flow = (
        small_flow(r.sx, r.sxbox, r.sxall), small_flow(r.sb, r.sbbox, r.sball),
        small_flow(r.sp, r.spbox, r.spall),
    )

    step(gain_flow, hid_flow, *wt_flows, *wx_flows)
    owned = [
        (r.hid_in, r.hid.at[q]), (r.gain_in, r.gain.at[d]),
        (tail_source(0, tail_rows), r.wt.at[d, pl.ds(0, tail_rows)]),
        (win_rows(inner, 0, width), r.wx.at[d]), (win_rows(0, 0, width), r.wz.at[d]),
        (r.og_in, r.og.at[q]),
    ]
    copies = [pltpu.make_async_copy(a, b, r.local.at[i]) for i, (a, b) in enumerate(owned)]
    for copy in copies:
        copy.start()

    @pl.when(d == q)
    def _():
        copy = pltpu.make_async_copy(r.wo_in, r.wo, r.local.at[len(owned)])
        copy.start()
        copy.wait()

    for i in range(dps):
        r.wt[i, tail_rows:, :] = jnp.zeros((r.wt.shape[1] - tail_rows, share), BF16)
    r.sx[...] = jnp.zeros_like(r.sx)
    r.sb[...] = jnp.zeros_like(r.sb)
    for copy in copies:
        copy.wait()
    finish(gain_flow)
    step(hid_flow, *wt_flows, *wx_flows)
    step(*wz_flows, og_flow)
    step(*wo_flows)
    hid_flow.finish()
    step(halo_flow)
    halo_flow.finish()

    gains = r.gain[0]
    for i in range(1, dps):
        gains = gains + r.gain[i]
    pre = gains[:, :model]
    r.pre_gain[...] = pre

    def normed(v):
        v = v.astype(F32)
        unit = v * lax.rsqrt(jnp.mean(v * v, -1, keepdims=True) + EPSILON)
        return (unit * pre).astype(BF16)

    def put_normed(at, rows, v):
        for i in range(dps):
            r.xn[i, pl.ds(at, rows), :] = v[:, i * share : (i + 1) * share]

    put_normed(0, HALO, jnp.where(p > 0, normed(r.halo[...]), jnp.zeros((HALO, model), BF16)))
    few = 32

    @pl.loop(0, tokens // few)
    def _(i):
        at = i * few
        rows = pl.ds(pl.multiple_of(at % piece, few), few)
        put_normed(pl.multiple_of(at + HALO, 16), few, normed(r.hid[at // piece, rows, :]))

    finish(*wt_flows, *wx_flows)

    def project(out_ref, out_at, at, rows, w_ref):
        total = jnp.zeros((rows, w_ref.shape[1]), F32)
        for i in range(dps):
            total = total + mm(r.xn[i, pl.ds(at, rows), :], w_ref[i], NT)
        out_ref[pl.ds(out_at, rows), :] = total.astype(BF16)

    for out_ref, w_ref in ((r.pt, r.wt), (r.px, r.wx)):
        project(out_ref, 0, 0, HALO, w_ref)

        @pl.loop(0, tokens // BLOCK)
        def _(i, out_ref=out_ref, w_ref=w_ref):
            at = pl.multiple_of(i * BLOCK + HALO, 16)
            project(out_ref, at, at, BLOCK, w_ref)

    pick = jnp.logical_and(lane_row == lane_col + q * own_heads, lane_col < own_heads).astype(BF16)
    r.pd[...] = mm(r.pt[:, state2 : state2 + 128], pick).astype(BF16)
    prep_pass(
        width, r.px, r.pt, r.pd, r.wxc, r.bxc, r.wbc, r.bbc, r.dtb, r.alog,
        r.xs, r.bc, r.dt, r.cum, r.fin, {0: lambda: step(*wz_flows, og_flow), 3: wo_flows[0].go},
    )
    step(state_flow)
    inside_pass(
        width, r.xs, r.bc, r.dt, r.cum, r.yl, {1: wo_flows[1].go, 3: wo_flows[2].go},
    )
    state_flow.finish()
    r.ds[...] = jnp.where(p > 0, r.enter[...], 0.0)
    outside_pass(
        width, r.xs, r.bc, r.dt, r.cum, r.skip, r.y, r.yl, r.states, r.ds, {1: wo_flows[3].go},
    )
    finish(*wz_flows)

    @pl.loop(0, tokens // BLOCK)
    def _(i):
        at = pl.multiple_of(i * BLOCK, BLOCK)
        project(r.z, at, pl.multiple_of(at + HALO, 16), BLOCK, r.wz)

    finish(og_flow, *wo_flows)

    @pl.loop(0, quads)
    def _(i):
        r.gm[pl.ds(pl.multiple_of(i * piece, piece), piece), :] = mm(r.og[i], r.wo[...], NT)

    norm_all = gains[:, model:]
    norm_own = norm_all[:, :width]
    for i in range(1, quads):
        norm_own = jnp.where(q == i, norm_all[:, i * width : (i + 1) * width], norm_own)
    chunk = 128

    @pl.loop(0, tokens // chunk)
    def _(i):
        rows = pl.ds(pl.multiple_of(i * chunk, chunk), chunk)
        gate = r.z[rows, :].astype(F32)
        gated = r.y[rows, :].astype(F32) * gate * sigmoid(gate)
        first = jnp.sum(gated * gated, -1, keepdims=True)
        second = jnp.sum(r.gm[rows, :] * norm_own * gated, -1, keepdims=True)
        lane = lax.broadcasted_iota(jnp.int32, (chunk, 128), 1)
        both = jnp.where(lane == 0, first, jnp.where(lane == 1, second, 0.0))
        r.stat[0, :, rows] = both.T[0:8, :]

    finish(stat_flow)

    @pl.loop(0, tokens // chunk)
    def _(i):
        rows = pl.ds(pl.multiple_of(i * chunk, chunk), chunk)
        stats = r.stat[len(up), :, rows]
        stats = jnp.concatenate([stats] * (128 // 8), 0).T
        out_rms = lax.rsqrt(stats[:, 0:1] / inner + EPSILON)
        mean_dot = out_rms * stats[:, 1:2] / inner
        gate = r.z[rows, :].astype(F32)
        y = r.y[rows, :].astype(F32)
        sig = sigmoid(gate)
        unit_gated = y * gate * sig * out_rms
        grad_mixed = r.gm[rows, :]
        r.mixed[rows, :] = (unit_gated * norm_own).astype(BF16)
        r.sx[5:6, :] += jnp.sum(grad_mixed * unit_gated, 0, keepdims=True)
        grad_gated = out_rms * (grad_mixed * norm_own - unit_gated * mean_dot)
        r.y[rows, :] = (grad_gated * gate * sig).astype(BF16)
        r.z[rows, :] = (grad_gated * y * sig * (1.0 + gate * (1.0 - sig))).astype(BF16)

    def weight_grad(grad_ref, out_ref):
        for i in range(dps):
            out_ref[i] = mm(grad_ref[...], r.xn[i, pl.ds(HALO, tokens), :], TN).astype(BF16)

    links.drain()

    @pl.loop(0, quads)
    def _(i):
        rows = pl.ds(pl.multiple_of(i * piece, piece), piece)
        r.hid[i] = mm(r.mixed[rows, :], r.wo[...]).astype(BF16)

    step(op_flow)
    weight_grad(r.z, r.grad)
    op_flow.go()
    step(*z_flows)
    leave_pass(width, r.bc, r.cum, r.y, r.fin)
    step(ds_flow)
    size = BLOCK if width % BLOCK == 0 else 128

    @pl.loop(0, width // size)
    def _(i):
        cols = pl.ds(pl.multiple_of(i * size, size), size)
        total = jnp.zeros((size, model), F32)
        for k in range(quads):
            total = total + mm(r.mixed[k * piece : (k + 1) * piece, cols], r.og[k], TN)
        r.wo[cols, :] = total.astype(BF16)

    step(*z_flows, *out_flows)
    back_inside_pass(width, r, {1: lambda: step(*z_flows)})
    ds_flow.finish()
    r.ds[...] = jnp.where(p > 0, 0.0, r.dsin[...])
    back_outside_pass(
        width, r, {1: lambda: step(*out_flows), 3: lambda: step(*out_flows)},
    )
    step(*edge_flows)
    r.sb[5:6, 0:128], r.sb[6:7, 0:128], r.sb[7:8, 0:128] = r.heads[0:1], r.heads[1:2], r.heads[2:3]
    op_flow.finish()
    op_flow.drain()
    for flow in z_flows:
        flow.drain()
    step(*z_flows)
    step(sx_flow, sb_flow)
    finish(*edge_flows)
    r.xs[pl.ds(tokens, 8), :] = jnp.where(p > 0, 0.0, r.hx[...])
    r.dbc[pl.ds(tokens, 8), :] = jnp.where(p > 0, 0.0, r.hb[...])

    def unconv(source, row, cols, w_ref):
        wide = source[pl.ds(row, chunk + 8), cols]
        total = jnp.zeros((chunk, 128), F32)
        for k in range(4):
            total = total + w_ref[k : k + 1, cols] * wide[3 - k : 3 - k + chunk]
        return total

    @pl.loop(0, tokens // chunk)
    def _(i):
        row = pl.multiple_of(i * chunk, chunk)
        inside = pl.ds(pl.multiple_of(row % piece, chunk), chunk)
        for c in range(2):
            cols = slice(128 * c, 128 * c + 128)
            r.bcs[row // piece, inside, cols] = unconv(r.dbc, row, cols, r.wbc)
        for pair in range(width // 128):
            cols = slice(128 * pair, 128 * pair + 128)
            r.mixed[pl.ds(row, chunk), cols] = unconv(r.xs, row, cols, r.wxc).astype(BF16)

    step(bc_flow)
    weight_grad(r.mixed, r.grad)
    for _ in dp_bits:
        step(sx_flow)
    step(*x_flows, bc_flow)
    row = lax.broadcasted_iota(jnp.int32, (state2, 128), 0)
    col = lax.broadcasted_iota(jnp.int32, (state2, 128), 1)
    from_bc = jnp.logical_and(row == col + q * bc_cols, col < bc_cols).astype(BF16)
    from_dt = jnp.logical_and(lane_col == lane_row + bc_cols, lane_row < own_heads).astype(BF16)

    wide_rows = r.wt.shape[1]
    row = lax.broadcasted_iota(jnp.int32, (128, wide_rows), 0)
    col = lax.broadcasted_iota(jnp.int32, (128, wide_rows), 1)

    def dt_rows(i):
        return jnp.logical_and(
            jnp.logical_and(row >= bc_cols, row < bc_cols + own_heads),
            col == state2 + i * own_heads + row - bc_cols,
        )

    def bc_rows(i):
        return jnp.logical_and(row < bc_cols, col == row + i * bc_cols)

    take = dt_rows(q).astype(BF16)
    for i in range(dps):
        r.wtail[i] = mm(take, r.wt[i]).astype(BF16)
    r.tail[...] = mm(r.gdt[...], from_dt).astype(BF16)
    r.sp[...] = jnp.zeros_like(r.sp)

    def grad_rows(k, carry):
        at = pl.multiple_of(k * chunk, chunk)
        rows = pl.ds(at, chunk)
        inside = pl.ds(pl.multiple_of(at % piece, chunk), chunk)
        gz, gx, gt = r.z[rows, :], r.mixed[rows, :], r.tail[rows, :]
        for i in range(dps):
            grad = mm(gz, r.wz[i]) + mm(gx, r.wx[i]) + mm(gt, r.wtail[i])
            cols = slice(i * share, (i + 1) * share)
            unit = r.xn[i, pl.ds(pl.multiple_of(at + HALO, 16), chunk), :].astype(F32)
            r.sp[:, cols] += jnp.sum(grad * unit, 0, keepdims=True)
            r.og[at // piece, inside, cols] = grad.astype(BF16)
        return carry

    lax.fori_loop(0, tokens // chunk, grad_rows, 0)
    step(gn_flow, bc_flow, *x_flows)
    step(gn_flow)
    finish(bc_flow)
    step(*x_flows)

    @pl.loop(0, quads)
    def _(i):
        rows = pl.ds(pl.multiple_of(i * piece, piece), piece)
        r.tail[rows, :] = (mm(r.bcall[i], from_bc) + mm(r.gdt[rows, :], from_dt)).astype(BF16)

    weight_grad(r.tail, r.gradt)
    step(t_flow, sb_flow, sx_flow, *out_flows)
    own_bc = r.bcall[q]
    for i in range(dps):
        cols = slice(i * share, (i + 1) * share)
        grad = mm(own_bc, r.wt[i, 0:state2, :])
        at = pl.ds(pl.multiple_of(q * piece + HALO, 16), piece)
        r.sp[:, cols] += jnp.sum(grad * r.xn[i, at, :].astype(F32), 0, keepdims=True)
        r.yl[i * piece : (i + 1) * piece, 0:share] = grad
    r.sp[...] = r.sp[...] / pre
    step(sp_flow)
    finish(t_flow, sp_flow, sx_flow, sb_flow, *z_flows, *out_flows, *x_flows, gn_flow)
    for i in range(dps):
        cols = slice(i * share, (i + 1) * share)
        r.gn_own[:, cols] += r.yl[i * piece : (i + 1) * piece, 0:share]

    for copy in kept:
        copy.wait()
    for i in range(quads):
        place = jnp.logical_or(bc_rows(i), dt_rows(i)).astype(BF16)
        piece_t = mm(place, r.ttot[i], TN)
        r.tstage[...] = piece_t.astype(BF16) if i == 0 else (r.tstage[...].astype(F32) + piece_t).astype(BF16)
    last = keeper(r.tstage.at[pl.ds(0, tail_rows)], r.in_out.at[pl.ds(2 * inner, tail_rows)], 12)
    last.start()
    for i in range(quads):
        cols = slice(i * width, (i + 1) * width)
        r.cxw[:, cols] = r.sxall[i, 0:4, :]
        r.cxb[:, cols] = r.sxall[i, 4:5, :]
        r.norm[:, cols] = r.sxall[i, 5:6, :]
    total = r.sball[0]
    every = r.spall[0]
    lane = lax.broadcasted_iota(jnp.int32, (8, 128), 1)
    packed = jnp.where(lane < own_heads, r.sball[0, :, 0:128], 0.0)
    for i in range(1, quads):
        total = total + r.sball[i]
        every = every + r.spall[i]
        moved = jnp.where(lane < own_heads, r.sball[i, :, 0:128], 0.0)
        packed = packed + pltpu.roll(moved, i * own_heads, 1)
    r.cbw[...] = total[0:4]
    r.cbb[...] = total[4:5]
    r.head[...] = packed
    r.pre[...] = every
    last.wait()
    links.drain()


def remote_call(kernel, ident, outs, any_inputs, any_outputs, scratch, flops=2 * 10**10):
    vmem, anywhere = pl.BlockSpec(memory_space=pltpu.VMEM), pl.BlockSpec(memory_space=pltpu.HBM)

    def run(*args):
        moved = sum(a.size * a.dtype.itemsize for a in (*args, *outs))
        return pl.pallas_call(
            kernel,
            out_shape=tuple(outs),
            in_specs=[anywhere if i in any_inputs else vmem for i in range(len(args))],
            out_specs=tuple([anywhere if i in any_outputs else vmem for i in range(len(outs))]),
            scratch_shapes=list(scratch),
            compiler_params=pltpu.CompilerParams(
                vmem_limit_bytes=67043328, collective_id=ident, has_side_effects=True
            ),
            cost_estimate=pl.CostEstimate(flops=flops, bytes_accessed=moved, transcendentals=0),
        )(*args)

    return run


def on_device(
    hidden_in, pre_gain, in_weight, conv_x_weight, conv_x_bias, conv_bc_weight, conv_bc_bias,
    dt_bias, a_log, skip, norm_gain, out_weight, output_gradient,
):
    dp, quads, rank = lax.axis_size("dp"), lax.axis_size("quad"), lax.axis_index("dp")
    quad = lax.axis_index("quad")
    _, local, model = hidden_in.shape
    inner, state2, heads = conv_x_bias.shape[0], conv_bc_bias.shape[0], dt_bias.shape[0]
    width, own_heads = inner // quads, heads // quads
    tokens, share, columns = local * quads, model // dp, in_weight.shape[1]

    def own(v, n, axis):
        return lax.dynamic_slice_in_dim(v, quad * n, n, axis)

    def spaced(v):
        return lax.dynamic_update_slice_in_dim(
            jnp.zeros((v.shape[0] * dp,), F32), v.astype(F32), rank * v.shape[0], 0
        )

    def pad_heads(v):
        return jnp.pad(own(v, own_heads, 0), (0, 128 - own_heads))[None]

    gain_row = jnp.concatenate([spaced(pre_gain), spaced(norm_gain)])[None]
    skip_own = jnp.repeat(own(skip, own_heads, 0), width // own_heads)[None]
    tail_rows = columns - 2 * inner
    tail_wide = tail_rows + -tail_rows % 128

    def sds(shape, dtype=F32):
        return jax.ShapeDtypeStruct(shape, dtype)

    def vm(*shape):
        return pltpu.VMEM(shape, F32)

    def vb(*shape):
        return pltpu.VMEM(shape, BF16)

    rows, own_out, steps = HALO + tokens, width // dp, len(bits_of(dp)) + 1
    levels = len(bits_of(quads))
    scratch = dict(
        wz=vb(dp, width, share), wx=vb(dp, width, share), wt=vb(dp, tail_wide, share),
        wo=vb(width, model), xn=vb(dp, rows, share), og=vb(quads, local, model),
        hid=vb(quads, local, model), px=vb(rows, width), pt=vb(rows, tail_wide), pd=vb(rows, 128),
        xs=vm(tokens + 8, width), bc=vm(tokens, state2), dt=vm(tokens, 128), cum=vm(tokens, 128),
        y=vb(tokens, width), yl=vm(tokens, width), states=vm(tokens // BLOCK, 128, width),
        z=vb(tokens, width), gm=vm(tokens, width), mixed=vb(tokens, width),
        dbc=vm(tokens + 8, state2), gdt=vb(tokens, 128), bcs=vm(quads, local, state2),
        bcbox=vm(quads - 1, local, state2), bcall=vb(quads, local, state2), tail=vb(tokens, 128),
        wtail=vb(dp, 128, share), grad=vb(dp, width, share), gradt=vb(dp, 128, share),
        zbox=vb(dp - 1, width, share), zpair=vb(width, share),
        xpair=vb(width, share),
        tbox=vb(dp - 1, 128, share), tpair=vb(128, share),
        obox=vb(2, dp - 1, own_out, model // 2), opair=vb(2, own_out, model // 2),
        opbox=vb(quads - 1, local, model),
        ttot=vb(quads, 128, share), tstage=vb(tail_wide, share),
        gain=vm(dp, *gain_row.shape), halo=vb(HALO, model), fin=vm(128, width), enter=vm(128, width),
        ds=vm(128, width), stat=vm(levels + 1, 8, tokens), statbox=vm(levels, 8, tokens),
        dscore=vm(BLOCK, BLOCK), heads=vm(8, 128), sx=vm(8, width), sb=vm(8, state2), sp=vm(1, model),
        sxbox=vm(steps, 8, width), sbbox=vm(steps, 8, state2), spbox=vm(steps, 1, model),
        sxall=vm(quads, 8, width), sball=vm(quads, 8, state2), spall=vm(quads, 1, model),
        hx=vm(8, width), hb=vm(8, state2), dsin=vm(128, width),
        send=pltpu.SemaphoreType.DMA((192,)), recv=pltpu.SemaphoreType.DMA((192,)),
        local=pltpu.SemaphoreType.DMA((16,)),
    )
    (
        in_out, out_out, op_own, gn_own, conv_x_grad, conv_x_bias_grad, norm_grad, conv_bc_grad,
        conv_bc_bias_grad, head_grad, pre_grad, pre_full,
    ) = remote_call(
        functools.partial(block_kernel, width, own_heads, heads), 0,
        [
            sds((columns, share), BF16), sds((quads, own_out, model), BF16), sds((local, model)),
            sds((local, model)), sds((4, inner)), sds((1, inner)), sds((1, inner)), sds((4, state2)),
            sds((1, state2)), sds((8, 128)), sds((1, model)), sds((1, model)),
        ],
        range(5), range(2), [scratch[name] for name in SCRATCH],
    )(
        in_weight.T, out_weight, hidden_in[0], output_gradient[0], gain_row,
        own(conv_x_weight, width, 1), own(conv_x_bias, width, 0)[None], conv_bc_weight,
        conv_bc_bias[None], pad_heads(dt_bias), pad_heads(a_log), skip_own,
    )
    wide = hidden_in[0].astype(F32)
    inv_rms = lax.rsqrt(jnp.mean(wide * wide, -1, keepdims=True) + EPSILON)
    unit_rows = wide * inv_rms
    unit_grad = gn_own * pre_full
    input_grad = output_gradient[0].astype(F32) + inv_rms * (
        unit_grad - unit_rows * jnp.mean(unit_grad * unit_rows, -1, keepdims=True)
    )
    return (
        (wide + op_own)[None], input_grad[None],
        lax.dynamic_slice_in_dim(pre_grad[0], rank * share, share, 0), in_out.T.astype(F32),
        conv_x_grad, conv_x_bias_grad[0], conv_bc_grad, conv_bc_bias_grad[0],
        head_grad[5, :heads], head_grad[6, :heads], head_grad[7, :heads],
        lax.dynamic_slice_in_dim(norm_grad[0], rank * (inner // dp), inner // dp, 0),
        out_out.reshape(width, model).astype(F32),
    )


def solution(mesh):
    dp, seq = mesh.shape["dp"], mesh.shape["seq"]
    fine = Mesh(mesh.devices.reshape(dp, 2, seq // 2), ("dp", "pair", "quad"))
    tokens, whole, rows = P("dp", ("pair", "quad"), None), P(), P("dp", None)
    return jax.shard_map(
        on_device,
        mesh=fine,
        in_specs=(
            tokens, P("dp"), rows, whole, whole, whole, whole, whole, whole, whole, P("dp"), rows, tokens,
        ),
        out_specs=(
            tokens, tokens, P("dp"), rows, whole, whole, whole, whole, whole, whole, whole, P("dp"), rows,
        ),
        check_vma=False,
    )
```

profile of v0, /device:TPU:0, one launch (start us, length us, event | category | flops | bytes accessed | tf_op | source)
XLA Modules:
  0.0 329.3 jit_solution(972977680224865864)
XLA Ops:
  0.7 0.8 convert_dynamic-update-slice_fusion
  1.5 0.8 convert_dynamic-update-slice_fusion.1
  2.2 0.6 broadcast_in_dim.34.refs_4_
  2.9 1.3 constant_dynamic-slice_fusion.refs_5_
  4.2 0.8 dynamic_slice.26
  4.9 0.6 broadcast_in_dim.35.refs_6_
  5.5 0.7 dynamic_slice.28
  6.3 0.7 dynamic_slice.27
  7.0 0.5 pad_bitcast_fusion
  7.5 0.7 dynamic_slice.29
  8.2 0.1 broadcast_in_dim.39
  8.3 0.7 broadcast_in_dim_reshape.3.refs_11_
  9.0 298.5 %shard_map.228 = (bf16[6448,384]{1,0:T(8,128)(2,1)}, bf16[4,192,1536]{2,1,0:T(8,128)(2,1)}, f32[256,1536]{1,0:T(8,128)}, f32[256,1536]{1,0:T(8,128)}, f32[4,3072...) custom-call(bf16[6448,384]{1,0:T(8,128)(2,1)} %bitcast.34, ...), custom_call_target="tpu_custom_call" | custom-call | flops 20000000000 | bytes 19479552 | tf_op jit(solution)/shard_map/pallas_call | solution.py:963
  307.4 0.7 reduce
  308.2 0.0 copy-start
  308.2 0.0 copy-start.1
  308.2 0.0 copy-start.4
  308.2 1.5 fusion.8
  309.7 2.0 fusion.2
  311.7 0.0 copy-done
  311.7 0.0 copy-done.1
  311.7 0.0 copy-done.4
  311.8 3.8 %fusion.6 = (f32[1,256,1536]{2,1,0:T(8,128)}, f32[1,256,1536]{2,1,0:T(8,128)}) fusion(f32[256,1536]{1,0:T(8,128)S(1)} %copy-done.1, f32[256]{0:T(256)S(1)} %broadcast_multiply_fusion, f32[1536]{0:T(1024)S(1)} %reduce, f32[256]{0:T(256)S(1)} %add_rsqrt_fusion, bf16[1,256,1536]{2,1,0:T(8,128)(2,1)S(1)} %copy-done.4, bf16[1,256,1536]{2,1,0:T(8,128)(2,1)S(1)} %copy-done, ...), kind=kLoop, calls=%fused_computation.11 | loop fusion | flops 3538944 | bytes 7872512 | tf_op jit(solution)/shard_map/broadcast_in_dim | solution.py:1065
  315.5 1.2 dynamic-slice_reduce_fusion.1
  316.7 4.5 %convert_bitcast_fusion = f32[384,6448]{0,1:T(8,128)} fusion(bf16[6448,384]{1,0:T(8,128)(2,1)S(1)} %copy-done.2), kind=kLoop, calls=%fused_computation | loop fusion | flops 2476032 | bytes 14856192 | tf_op jit(solution)/shard_map/convert_element_type | solution.py:1066
  321.3 1.3 slice_bitcast_fusion
  322.6 1.3 dynamic-slice_reduce_fusion
  323.9 3.0 bitcast_convert_fusion
  326.9 0.6 copy.32
  327.5 0.6 copy.33
  328.1 0.6 copy.34
  328.7 0.6 copy.35
  (17 shorter events, 0.1 us)
Async XLA Ops:
  308.2 3.6 %copy-start = (bf16[1,256,1536]{2,1,0:T(8,128)(2,1)S(1)}, bf16[1,256,1536]{2,1,0:T(8,128)(2,1)}, u32[]{:S(2)}) copy-start(bf16[1,256,1536]{2,1,0:T(8,128)(2,1)} %param.13) | copy-start | bytes 2359300
  308.2 3.6 %copy-start.1 = (f32[256,1536]{1,0:T(8,128)S(1)}, f32[256,1536]{1,0:T(8,128)}, u32[]{:S(2)}) copy-start(f32[256,1536]{1,0:T(8,128)} %get-tuple-element.26) | copy-start | bytes 4718596
  308.2 3.6 %copy-start.4 = (bf16[1,256,1536]{2,1,0:T(8,128)(2,1)S(1)}, bf16[1,256,1536]{2,1,0:T(8,128)(2,1)}, u32[]{:S(2)}) copy-start(bf16[1,256,1536]{2,1,0:T(8,128)(2,1)} %param.25) | copy-start | bytes 2359300
  311.7 5.0 %copy-start.2 = (bf16[6448,384]{1,0:T(8,128)(2,1)S(1)}, bf16[6448,384]{1,0:T(8,128)(2,1)}, u32[]{:S(2)}) copy-start(bf16[6448,384]{1,0:T(8,128)(2,1)} %get-tuple-element.29) | copy-start | bytes 14856196
  316.7 7.1 %copy-start.3 = (bf16[4,192,1536]{2,1,0:T(8,128)(2,1)S(1)}, bf16[4,192,1536]{2,1,0:T(8,128)(2,1)}, u32[]{:S(2)}) copy-start(bf16[4,192,1536]{2,1,0:T(8,128)(2,1)} %get-tuple-element.36) | copy-start | bytes 7077892
  323.9 3.0 copy-start.5
  323.9 3.6 %copy-start.6 = (f32[1,3072]{1,0:T(1,128)S(1)}, f32[1,3072]{1,0:T(1,128)}, u32[]{:S(2)}) copy-start(f32[1,3072]{1,0:T(1,128)} %get-tuple-element.31) | copy-start | bytes 36868
  323.9 4.2 %copy-start.7 = (f32[4,256]{1,0:T(4,128)S(1)}, f32[4,256]{1,0:T(4,128)}, u32[]{:S(2)}) copy-start(f32[4,256]{1,0:T(4,128)} %get-tuple-element.63) | copy-start | bytes 12292
  323.9 4.8 %copy-start.8 = (f32[1,256]{1,0:T(1,128)S(1)}, f32[1,256]{1,0:T(1,128)}, u32[]{:S(2)}) copy-start(f32[1,256]{1,0:T(1,128)} %get-tuple-element.33) | copy-start | bytes 3076
where the time goes:
time: 334 us; the launch traced here: 329 us
  Pallas kernels  298 us (89%)
  other arithmetic  17.1 us (5%)
  local copies, waits for them, and re-layouts  12.9 us (4%)
    pallas_call x1, Pallas kernels, run(): pl.pallas_call(kernel, out_shape=tuple(outs), in_specs=[anywhere if i in...  298 us

commit v1 on v0

--- a/solution.py
+++ b/solution.py
@@ -294,6 +294,8 @@
 def add_rows(out, a, b):
     rows = out.shape[0]
     step = 16 if rows % 16 == 0 else 8
+    while out.shape[1] * step * 2 <= 24576 and rows % (2 * step) == 0:
+        step *= 2
 
     @pl.loop(0, rows // step)
     def _(i):
@@ -479,13 +481,13 @@
 
 
 INPUTS = (
-    "win", "wo_in", "hid_in", "og_in", "gain_in", "wxc", "bxc", "wbc", "bbc", "dtb", "alog", "skip",
+    "win", "wo_in", "hid_in", "og_in", "gain_in", "wx_all", "bx_all", "wbc", "bbc", "per_head",
 )
 OUTPUTS = (
-    "in_out", "out_out", "op_own", "gn_own", "cxw", "cxb", "norm", "cbw", "cbb", "head", "pre", "pre_gain",
+    "in_out", "out_out", "op_own", "gn_own", "cxw", "cxb", "norm", "cbw", "cbb", "head", "pre",
 )
 SCRATCH = (
-    "wz", "wx", "wt", "wo", "xn", "og", "hid", "px", "pt", "pd", "xs", "bc", "dt", "cum", "y", "yl", "states", "z", "gm", "mixed", "dbc", "gdt", "bcs", "bcbox", "bcall", "tail", "wtail", "grad", "gradt", "zbox", "zpair", "xpair", "tbox", "tpair", "obox", "opair", "opbox", "ttot", "tstage", "gain", "halo", "fin", "enter", "ds", "stat", "statbox", "dscore", "heads", "sx", "sb", "sp", "sxbox", "sbbox", "spbox", "sxall", "sball", "spall", "hx", "hb", "dsin", "send", "recv", "local",
+    "wz", "wx", "wt", "wo", "xn", "og", "hid", "px", "pt", "pd", "xs", "bc", "dt", "cum", "y", "yl", "states", "z", "gm", "mixed", "dbc", "gdt", "bcs", "bcbox", "bcall", "tail", "wtail", "grad", "gradt", "zbox", "zpair", "xpair", "tbox", "tpair", "obox", "opair", "opbox", "ttot", "tstage", "gain", "halo", "fin", "enter", "ds", "stat", "statbox", "dscore", "heads", "sx", "sb", "sp", "sxbox", "sbbox", "spbox", "sxall", "sball", "spall", "hx", "hb", "dsin", "hown", "oown", "wxc", "bxc", "dtb", "alog", "skip", "send", "recv", "local",
 )
 
 
@@ -677,6 +679,22 @@
         r.wt[i, tail_rows:, :] = jnp.zeros((r.wt.shape[1] - tail_rows, share), BF16)
     r.sx[...] = jnp.zeros_like(r.sx)
     r.sb[...] = jnp.zeros_like(r.sb)
+    own_cols = pl.ds(pl.multiple_of(q * width, 128), width)
+    r.wxc[...] = r.wx_all[:, own_cols]
+    r.bxc[...] = r.bx_all[:, own_cols]
+    turned = r.per_head[...]
+    for i in range(1, quads):
+        turned = jnp.where(q == i, pltpu.roll(r.per_head[...], 128 - i * own_heads, 1), turned)
+    r.dtb[...] = turned[0:1]
+    r.alog[...] = turned[1:2]
+    head_row = lax.broadcasted_iota(jnp.int32, (128, width), 0)
+    head_col = lax.broadcasted_iota(jnp.int32, (128, width), 1)
+    widen = (head_row == head_col // (width // own_heads)).astype(BF16)
+    s0 = turned.astype(BF16)
+    rest = turned - s0.astype(F32)
+    s1 = rest.astype(BF16)
+    s2 = (rest - s1.astype(F32)).astype(BF16)
+    r.skip[...] = (mm(s0, widen) + mm(s1, widen) + mm(s2, widen))[2:3]
     for copy in copies:
         copy.wait()
     finish(gain_flow)
@@ -691,7 +709,6 @@
     for i in range(1, dps):
         gains = gains + r.gain[i]
     pre = gains[:, :model]
-    r.pre_gain[...] = pre
 
     def normed(v):
         v = v.astype(F32)
@@ -737,18 +754,18 @@
     inside_pass(
         width, r.xs, r.bc, r.dt, r.cum, r.yl, {1: wo_flows[1].go, 3: wo_flows[2].go},
     )
+    finish(*wz_flows)
+
+    @pl.loop(0, tokens // BLOCK)
+    def _(i):
+        at = pl.multiple_of(i * BLOCK, BLOCK)
+        project(r.z, at, pl.multiple_of(at + HALO, 16), BLOCK, r.wz)
+
     state_flow.finish()
     r.ds[...] = jnp.where(p > 0, r.enter[...], 0.0)
     outside_pass(
         width, r.xs, r.bc, r.dt, r.cum, r.skip, r.y, r.yl, r.states, r.ds, {1: wo_flows[3].go},
     )
-    finish(*wz_flows)
-
-    @pl.loop(0, tokens // BLOCK)
-    def _(i):
-        at = pl.multiple_of(i * BLOCK, BLOCK)
-        project(r.z, at, pl.multiple_of(at + HALO, 16), BLOCK, r.wz)
-
     finish(og_flow, *wo_flows)
 
     @pl.loop(0, quads)
@@ -803,6 +820,12 @@
         rows = pl.ds(pl.multiple_of(i * piece, piece), piece)
         r.hid[i] = mm(r.mixed[rows, :], r.wo[...]).astype(BF16)
 
+    own_copies = [
+        pltpu.make_async_copy(a, b, r.local.at[i])
+        for i, (a, b) in enumerate(((r.hid_in, r.hown), (r.og_in, r.oown)))
+    ]
+    for copy in own_copies:
+        copy.start()
     step(op_flow)
     weight_grad(r.z, r.grad)
     op_flow.go()
@@ -820,20 +843,14 @@
         r.wo[cols, :] = total.astype(BF16)
 
     step(*z_flows, *out_flows)
+    blocks = tokens // BLOCK
     back_inside_pass(width, r, {1: lambda: step(*z_flows)})
     ds_flow.finish()
     r.ds[...] = jnp.where(p > 0, 0.0, r.dsin[...])
     back_outside_pass(
-        width, r, {1: lambda: step(*out_flows), 3: lambda: step(*out_flows)},
+        width, r, {1: lambda: step(*out_flows), blocks - 1: lambda: step(*edge_flows, *out_flows)},
     )
-    step(*edge_flows)
     r.sb[5:6, 0:128], r.sb[6:7, 0:128], r.sb[7:8, 0:128] = r.heads[0:1], r.heads[1:2], r.heads[2:3]
-    op_flow.finish()
-    op_flow.drain()
-    for flow in z_flows:
-        flow.drain()
-    step(*z_flows)
-    step(sx_flow, sb_flow)
     finish(*edge_flows)
     r.xs[pl.ds(tokens, 8), :] = jnp.where(p > 0, 0.0, r.hx[...])
     r.dbc[pl.ds(tokens, 8), :] = jnp.where(p > 0, 0.0, r.hb[...])
@@ -856,6 +873,12 @@
             cols = slice(128 * pair, 128 * pair + 128)
             r.mixed[pl.ds(row, chunk), cols] = unconv(r.xs, row, cols, r.wxc).astype(BF16)
 
+    op_flow.finish()
+    op_flow.drain()
+    for flow in z_flows:
+        flow.drain()
+    step(*z_flows)
+    step(sx_flow, sb_flow)
     step(bc_flow)
     weight_grad(r.mixed, r.grad)
     for _ in dp_bits:
@@ -899,10 +922,11 @@
         return carry
 
     lax.fori_loop(0, tokens // chunk, grad_rows, 0)
-    step(gn_flow, bc_flow, *x_flows)
-    step(gn_flow)
+    step(gn_flow, *x_flows)
+    step(bc_flow, gn_flow)
+    step(*x_flows)
+    step(*out_flows)
     finish(bc_flow)
-    step(*x_flows)
 
     @pl.loop(0, quads)
     def _(i):
@@ -910,7 +934,7 @@
         r.tail[rows, :] = (mm(r.bcall[i], from_bc) + mm(r.gdt[rows, :], from_dt)).astype(BF16)
 
     weight_grad(r.tail, r.gradt)
-    step(t_flow, sb_flow, sx_flow, *out_flows)
+    step(t_flow, sb_flow, sx_flow)
     own_bc = r.bcall[q]
     for i in range(dps):
         cols = slice(i * share, (i + 1) * share)
@@ -919,11 +943,28 @@
         r.sp[:, cols] += jnp.sum(grad * r.xn[i, at, :].astype(F32), 0, keepdims=True)
         r.yl[i * piece : (i + 1) * piece, 0:share] = grad
     r.sp[...] = r.sp[...] / pre
-    step(sp_flow)
-    finish(t_flow, sp_flow, sx_flow, sb_flow, *z_flows, *out_flows, *x_flows, gn_flow)
+    step(sp_flow, t_flow, *out_flows)
+    step(sp_flow, t_flow)
+    step(*z_flows)
+    step(sp_flow, sx_flow, sb_flow, *out_flows)
+    finish(*x_flows, t_flow, sp_flow, *out_flows, *z_flows, sx_flow, sb_flow, gn_flow)
+    for copy in own_copies:
+        copy.wait()
     for i in range(dps):
         cols = slice(i * share, (i + 1) * share)
         r.gn_own[:, cols] += r.yl[i * piece : (i + 1) * piece, 0:share]
+
+    @pl.loop(0, piece // few)
+    def _(i):
+        rows = pl.ds(pl.multiple_of(i * few, few), few)
+        wide = r.hown[rows, :].astype(F32)
+        r.op_own[rows, :] = wide + r.op_own[rows, :]
+        inv_rms = lax.rsqrt(jnp.mean(wide * wide, -1, keepdims=True) + EPSILON)
+        unit = wide * inv_rms
+        grad = r.gn_own[rows, :] * pre
+        r.gn_own[rows, :] = r.oown[rows, :].astype(F32) + inv_rms * (
+            grad - unit * jnp.mean(grad * unit, -1, keepdims=True)
+        )
 
     for copy in kept:
         copy.wait()
@@ -980,25 +1021,18 @@
     dt_bias, a_log, skip, norm_gain, out_weight, output_gradient,
 ):
     dp, quads, rank = lax.axis_size("dp"), lax.axis_size("quad"), lax.axis_index("dp")
-    quad = lax.axis_index("quad")
     _, local, model = hidden_in.shape
     inner, state2, heads = conv_x_bias.shape[0], conv_bc_bias.shape[0], dt_bias.shape[0]
     width, own_heads = inner // quads, heads // quads
     tokens, share, columns = local * quads, model // dp, in_weight.shape[1]
 
-    def own(v, n, axis):
-        return lax.dynamic_slice_in_dim(v, quad * n, n, axis)
-
     def spaced(v):
         return lax.dynamic_update_slice_in_dim(
             jnp.zeros((v.shape[0] * dp,), F32), v.astype(F32), rank * v.shape[0], 0
         )
 
-    def pad_heads(v):
-        return jnp.pad(own(v, own_heads, 0), (0, 128 - own_heads))[None]
-
     gain_row = jnp.concatenate([spaced(pre_gain), spaced(norm_gain)])[None]
-    skip_own = jnp.repeat(own(skip, own_heads, 0), width // own_heads)[None]
+    per_head = jnp.pad(jnp.stack([dt_bias, a_log, skip]), ((0, 5), (0, 128 - heads)))
     tail_rows = columns - 2 * inner
     tail_wide = tail_rows + -tail_rows % 128
 
@@ -1034,35 +1068,28 @@
         dscore=vm(BLOCK, BLOCK), heads=vm(8, 128), sx=vm(8, width), sb=vm(8, state2), sp=vm(1, model),
         sxbox=vm(steps, 8, width), sbbox=vm(steps, 8, state2), spbox=vm(steps, 1, model),
         sxall=vm(quads, 8, width), sball=vm(quads, 8, state2), spall=vm(quads, 1, model),
-        hx=vm(8, width), hb=vm(8, state2), dsin=vm(128, width),
+        hx=vm(8, width), hb=vm(8, state2), dsin=vm(128, width), hown=vb(local, model), oown=vb(local, model),
+        wxc=vm(4, width), bxc=vm(1, width), dtb=vm(1, 128), alog=vm(1, 128), skip=vm(1, width),
         send=pltpu.SemaphoreType.DMA((192,)), recv=pltpu.SemaphoreType.DMA((192,)),
         local=pltpu.SemaphoreType.DMA((16,)),
     )
     (
         in_out, out_out, op_own, gn_own, conv_x_grad, conv_x_bias_grad, norm_grad, conv_bc_grad,
-        conv_bc_bias_grad, head_grad, pre_grad, pre_full,
+        conv_bc_bias_grad, head_grad, pre_grad,
     ) = remote_call(
         functools.partial(block_kernel, width, own_heads, heads), 0,
         [
             sds((columns, share), BF16), sds((quads, own_out, model), BF16), sds((local, model)),
             sds((local, model)), sds((4, inner)), sds((1, inner)), sds((1, inner)), sds((4, state2)),
-            sds((1, state2)), sds((8, 128)), sds((1, model)), sds((1, model)),
+            sds((1, state2)), sds((8, 128)), sds((1, model)),
         ],
         range(5), range(2), [scratch[name] for name in SCRATCH],
     )(
-        in_weight.T, out_weight, hidden_in[0], output_gradient[0], gain_row,
-        own(conv_x_weight, width, 1), own(conv_x_bias, width, 0)[None], conv_bc_weight,
-        conv_bc_bias[None], pad_heads(dt_bias), pad_heads(a_log), skip_own,
-    )
-    wide = hidden_in[0].astype(F32)
-    inv_rms = lax.rsqrt(jnp.mean(wide * wide, -1, keepdims=True) + EPSILON)
-    unit_rows = wide * inv_rms
-    unit_grad = gn_own * pre_full
-    input_grad = output_gradient[0].astype(F32) + inv_rms * (
-        unit_grad - unit_rows * jnp.mean(unit_grad * unit_rows, -1, keepdims=True)
+        in_weight.T, out_weight, hidden_in[0], output_gradient[0], gain_row, conv_x_weight,
+        conv_x_bias[None], conv_bc_weight, conv_bc_bias[None], per_head,
     )
     return (
-        (wide + op_own)[None], input_grad[None],
+        op_own[None], gn_own[None],
         lax.dynamic_slice_in_dim(pre_grad[0], rank * share, share, 0), in_out.T.astype(F32),
         conv_x_grad, conv_x_bias_grad[0], conv_bc_grad, conv_bc_bias_grad[0],
         head_grad[5, :heads], head_grad[6, :heads], head_grad[7, :heads],

time: 334 us -> 323 us (0.967); the launches traced: 329 us -> 322 us
  other arithmetic: 17.1 us -> 12.9 us
  local copies, waits for them, and re-layouts: 12.9 us -> 9.19 us
    dynamic_slice x5 -> x0, local copies, waits for them, and re-layouts: 4.26 us -> none  [own(): return lax.dynamic_slice_in_dim(v, quad * n, n, axis)]
    broadcast_in_dim x1 -> x0, other arithmetic: 3.77 us -> none  [on_device(): input_grad[None]]
    reduce_sum x2 -> x0, other arithmetic: 3.51 us -> none  [the longest x1 2 us: on_device(): jnp.mean(unit_grad * unit_rows, -1, keepdims=True)]
where the time goes in v1:
time: 323 us; the launch traced here: 322 us
  Pallas kernels  299 us (93%)
  other arithmetic  12.9 us (4%)
  local copies, waits for them, and re-layouts  9.19 us (3%)
    pallas_call x1, Pallas kernels, run(): pl.pallas_call(kernel, out_shape=tuple(outs), in_specs=[anywhere if i in...  299 us
    convert_element_type x1, other arithmetic, on_device(): in_out.T.astype(F32)  7.09 us

profile of v1, /device:TPU:0, one launch (start us, length us, event | category | flops | bytes accessed | tf_op | source)
XLA Modules:
  0.0 322.0 jit_solution(16138161768127485914)
XLA Ops:
  0.7 0.8 convert_dynamic-update-slice_fusion
  1.5 0.8 convert_dynamic-update-slice_fusion.1
  2.2 0.6 broadcast_in_dim.23.refs_4_
  2.9 1.3 select_maximum_fusion.refs_9_
  4.2 299.2 %shard_map.228 = (bf16[6448,384]{1,0:T(8,128)(2,1)}, bf16[4,192,1536]{2,1,0:T(8,128)(2,1)}, f32[256,1536]{1,0:T(8,128)}, f32[256,1536]{1,0:T(8,128)}, f32[4,3072...) custom-call(bf16[6448,384]{1,0:T(8,128)(2,1)} %bitcast.30, ...), custom_call_target="tpu_custom_call" | custom-call | flops 20000000000 | bytes 19519488 | tf_op jit(solution)/shard_map/pallas_call | solution.py:1004
  303.4 1.3 dynamic-slice_reduce_fusion
  304.7 1.3 dynamic-slice_reduce_fusion.1
  305.9 1.3 slice_bitcast_fusion
  307.3 0.0 copy-start
  307.3 7.1 %convert_bitcast_fusion = f32[384,6448]{0,1:T(8,128)} fusion(bf16[6448,384]{1,0:T(8,128)(2,1)} %get-tuple-element.27), kind=kLoop, calls=%fused_computation | loop fusion | flops 2476032 | bytes 14856192 | tf_op jit(solution)/shard_map/convert_element_type | solution.py:1093
  314.3 0.0 copy-start.2
  314.3 0.0 copy-done
  314.3 0.0 copy-start.1
  314.3 3.0 bitcast_convert_fusion
  317.3 0.0 copy-start.3
  317.3 0.0 copy-start.4
  317.3 0.0 copy-start.5
  317.3 0.0 copy-start.6
  317.3 0.0 copy-done.2
  317.4 1.1 copy.34
  318.5 0.0 copy-done.1
  318.5 1.1 copy.35
  319.6 0.0 copy-done.3
  319.6 0.6 copy.36
  320.3 0.0 copy-done.4
  320.3 0.6 copy.37
  320.9 0.0 copy-done.5
  320.9 0.6 copy.38
  321.5 0.0 copy-done.6
  321.5 0.6 copy.39
  (3 shorter events, 0.0 us)
Async XLA Ops:
  307.3 7.1 %copy-start = (bf16[4,192,1536]{2,1,0:T(8,128)(2,1)S(1)}, bf16[4,192,1536]{2,1,0:T(8,128)(2,1)}, u32[]{:S(2)}) copy-start(bf16[4,192,1536]{2,1,0:T(8,128)(2,1)} %get-tuple-element.34) | copy-start | bytes 7077892
  314.3 3.0 copy-start.2
  314.3 4.2 %copy-start.1 = (f32[256,1536]{1,0:T(8,128)S(1)}, f32[256,1536]{1,0:T(8,128)}, u32[]{:S(2)}) copy-start(f32[256,1536]{1,0:T(8,128)} %get-tuple-element.25) | copy-start | bytes 4718596
  317.3 2.3 copy-start.3
  317.3 2.9 copy-start.4
  317.3 3.5 %copy-start.5 = (f32[4,256]{1,0:T(4,128)S(1)}, f32[4,256]{1,0:T(4,128)}, u32[]{:S(2)}) copy-start(f32[4,256]{1,0:T(4,128)} %get-tuple-element.57) | copy-start | bytes 12292
  317.3 4.1 %copy-start.6 = (f32[1,256]{1,0:T(1,128)S(1)}, f32[1,256]{1,0:T(1,128)}, u32[]{:S(2)}) copy-start(f32[1,256]{1,0:T(1,128)} %get-tuple-element.31) | copy-start | bytes 3076

commit v2 on v1

--- a/solution.py
+++ b/solution.py
@@ -908,24 +908,25 @@
     r.tail[...] = mm(r.gdt[...], from_dt).astype(BF16)
     r.sp[...] = jnp.zeros_like(r.sp)
 
+    span = min(BLOCK, piece)
+
     def grad_rows(k, carry):
-        at = pl.multiple_of(k * chunk, chunk)
-        rows = pl.ds(at, chunk)
-        inside = pl.ds(pl.multiple_of(at % piece, chunk), chunk)
+        at = pl.multiple_of(k * span, span)
+        rows = pl.ds(at, span)
+        inside = pl.ds(pl.multiple_of(at % piece, span), span)
         gz, gx, gt = r.z[rows, :], r.mixed[rows, :], r.tail[rows, :]
         for i in range(dps):
             grad = mm(gz, r.wz[i]) + mm(gx, r.wx[i]) + mm(gt, r.wtail[i])
             cols = slice(i * share, (i + 1) * share)
-            unit = r.xn[i, pl.ds(pl.multiple_of(at + HALO, 16), chunk), :].astype(F32)
+            unit = r.xn[i, pl.ds(pl.multiple_of(at + HALO, 16), span), :].astype(F32)
             r.sp[:, cols] += jnp.sum(grad * unit, 0, keepdims=True)
             r.og[at // piece, inside, cols] = grad.astype(BF16)
         return carry
 
-    lax.fori_loop(0, tokens // chunk, grad_rows, 0)
+    lax.fori_loop(0, tokens // span, grad_rows, 0)
     step(gn_flow, *x_flows)
-    step(bc_flow, gn_flow)
+    step(bc_flow, *out_flows, gn_flow)
     step(*x_flows)
-    step(*out_flows)
     finish(bc_flow)
 
     @pl.loop(0, quads)
@@ -947,7 +948,7 @@
     step(sp_flow, t_flow)
     step(*z_flows)
     step(sp_flow, sx_flow, sb_flow, *out_flows)
-    finish(*x_flows, t_flow, sp_flow, *out_flows, *z_flows, sx_flow, sb_flow, gn_flow)
+    gn_flow.finish()
     for copy in own_copies:
         copy.wait()
     for i in range(dps):
@@ -966,6 +967,7 @@
             grad - unit * jnp.mean(grad * unit, -1, keepdims=True)
         )
 
+    finish(*x_flows, t_flow, sp_flow, *out_flows, *z_flows, sx_flow, sb_flow)
     for copy in kept:
         copy.wait()
     for i in range(quads):

time: 323 us -> 324 us (level)
  no operation moved by 1% of the time
where the time goes in v2:
time: 324 us; the launch traced here: 321 us
  Pallas kernels  298 us (92%)
  other arithmetic  12.9 us (4%)
  local copies, waits for them, and re-layouts  9.19 us (3%)
    pallas_call x1, Pallas kernels, run(): pl.pallas_call(kernel, out_shape=tuple(outs), in_specs=[anywhere if i in...  298 us
    convert_element_type x1, other arithmetic, on_device(): in_out.T.astype(F32)  7.09 us

profile of v2, /device:TPU:0, one launch (start us, length us, event | category | flops | bytes accessed | tf_op | source)
XLA Modules:
  0.0 320.7 jit_solution(17417926737423769468)
XLA Ops:
  0.7 0.8 convert_dynamic-update-slice_fusion
  1.5 0.8 convert_dynamic-update-slice_fusion.1
  2.2 0.6 broadcast_in_dim.23.refs_4_
  2.9 1.3 select_maximum_fusion.refs_9_
  4.2 297.9 %shard_map.228 = (bf16[6448,384]{1,0:T(8,128)(2,1)}, bf16[4,192,1536]{2,1,0:T(8,128)(2,1)}, f32[256,1536]{1,0:T(8,128)}, f32[256,1536]{1,0:T(8,128)}, f32[4,3072...) custom-call(bf16[6448,384]{1,0:T(8,128)(2,1)} %bitcast.30, ...), custom_call_target="tpu_custom_call" | custom-call | flops 20000000000 | bytes 19519488 | tf_op jit(solution)/shard_map/pallas_call | solution.py:1006
  302.1 1.3 dynamic-slice_reduce_fusion
  303.4 1.3 dynamic-slice_reduce_fusion.1
  304.7 1.3 slice_bitcast_fusion
  306.0 0.0 copy-start
  306.0 7.1 %convert_bitcast_fusion = f32[384,6448]{0,1:T(8,128)} fusion(bf16[6448,384]{1,0:T(8,128)(2,1)} %get-tuple-element.27), kind=kLoop, calls=%fused_computation | loop fusion | flops 2476032 | bytes 14856192 | tf_op jit(solution)/shard_map/convert_element_type | solution.py:1095
  313.1 0.0 copy-start.2
  313.1 0.0 copy-done
  313.1 0.0 copy-start.1
  313.1 3.0 bitcast_convert_fusion
  316.0 0.0 copy-start.3
  316.0 0.0 copy-start.4
  316.0 0.0 copy-start.5
  316.0 0.0 copy-start.6
  316.1 0.0 copy-done.2
  316.1 1.1 copy.34
  317.2 0.0 copy-done.1
  317.2 1.1 copy.35
  318.4 0.0 copy-done.3
  318.4 0.6 copy.36
  319.0 0.0 copy-done.4
  319.0 0.6 copy.37
  319.6 0.0 copy-done.5
  319.6 0.6 copy.38
  320.2 0.0 copy-done.6
  320.2 0.6 copy.39
  (3 shorter events, 0.0 us)
Async XLA Ops:
  306.0 7.1 %copy-start = (bf16[4,192,1536]{2,1,0:T(8,128)(2,1)S(1)}, bf16[4,192,1536]{2,1,0:T(8,128)(2,1)}, u32[]{:S(2)}) copy-start(bf16[4,192,1536]{2,1,0:T(8,128)(2,1)} %get-tuple-element.34) | copy-start | bytes 7077892
  313.1 3.0 copy-start.2
  313.1 4.2 %copy-start.1 = (f32[256,1536]{1,0:T(8,128)S(1)}, f32[256,1536]{1,0:T(8,128)}, u32[]{:S(2)}) copy-start(f32[256,1536]{1,0:T(8,128)} %get-tuple-element.25) | copy-start | bytes 4718596
  316.0 2.3 copy-start.3
  316.0 2.9 copy-start.4
  316.0 3.5 %copy-start.5 = (f32[4,256]{1,0:T(4,128)S(1)}, f32[4,256]{1,0:T(4,128)}, u32[]{:S(2)}) copy-start(f32[4,256]{1,0:T(4,128)} %get-tuple-element.57) | copy-start | bytes 12292
  316.0 4.1 %copy-start.6 = (f32[1,256]{1,0:T(1,128)S(1)}, f32[1,256]{1,0:T(1,128)}, u32[]{:S(2)}) copy-start(f32[1,256]{1,0:T(1,128)} %get-tuple-element.31) | copy-start | bytes 3076
